TPU v7x, 256 devices: a whole 4x4x8 slice. The times are simulated.
256 devices in a mesh: ctx: 8 (over z), vocab: 32 (over y, x, core).
Axes of the slice: x: 4, y: 4, z: 8, core: 2. Of those that a mesh axis runs over, the one named last changes fastest.
Arguments:
- hidden: bfloat16 [16, 128, 4096], P(None, 'ctx', 'vocab'), may hold values from -6 to 6
- head_weight: bfloat16 [4096, 128256], P(None, ('ctx', 'vocab')), may hold values from -0.09375 to 0.09375
- token_ids: int32 [16, 128], P(None, 'ctx'), may hold values from 0 to 128255
- response_mask: int32 [16, 128], P(None, 'ctx'), may hold values 0 or 1
- pair_order: int32 [16], replicated, may hold values from 0 to 15, each once
- frozen_logprob: float32 [16], replicated, may hold values from -40 to 40
Outputs:
- pair_loss: float32 [], replicated
- margins: float32 [8], replicated
- head_grad: bfloat16 [4096, 128256], P(None, ('ctx', 'vocab'))
- spread_grad: bfloat16 [4096, 128256], P(None, ('ctx', 'vocab'))
Inputs may be any that keep to these rules, and one draw needn't show every extreme that they name: `token_ids`: token ids lie in 0 to 128255. `response_mask`: mask entries are 0 or 1. pair_order names every sequence exactly once; entry p is the chosen sequence of pair p and entry 8 + p the rejected one.
All inputs are finite; a program needn't handle non-finite values.
Results may differ from a plain program's by a relative error of at most 0.0015.
Values may be sent and summed in bfloat16 or wider, within the bound.
A program may use at most 128 MiB of HBM per device.

v0:
```python
import jax
import jax.numpy as jnp
from jax import lax
from jax.sharding import Mesh
from jax.sharding import PartitionSpec as P

V = 128256
VOCAB = ("vocab_0", "vocab_1", "vocab_2")
CTX_VOCAB = ("ctx", "vocab_0", "vocab_1", "vocab_2")
strength = 0.1
loss_scale = 256.0


def laid_out(pieces, dim):
    pieces = jnp.moveaxis(pieces, 0, dim)
    lengths = pieces.shape
    return pieces.reshape(*lengths[:dim], lengths[dim] * lengths[dim + 1], *lengths[dim + 2 :])


def gather_packed(arrays, axis, dims):
    flat = jnp.concatenate([a.reshape(-1) for a in arrays])
    lines, at, finished = (lax.all_gather(flat, axis), 0, [])
    for a, dim in zip(arrays, dims):
        pieces = lines[:, at : at + a.size].reshape(-1, *a.shape)
        finished.append(laid_out(pieces, dim))
        at += a.size
    return tuple(finished)


def by_axis(shard, axes):
    for axis in axes:
        shard = lax.pmax(shard, axis)
    return shard


def by_axis_2(shard, axes):
    for axis in axes:
        shard = lax.psum(shard, axis)
    return shard


def contract_rows(block_rows, both_logits):
    return lax.dot_general(
        block_rows, both_logits, (((0,), (0,)), ((), ())), preferred_element_type=jnp.float32
    )


def shards(hidden, head_weight, token_ids, response_mask, pair_order, frozen_logprob):
    seq_rows = lax.all_gather(hidden, "ctx", axis=1, tiled=True)
    ids_all, mask_all = gather_packed((token_ids, response_mask), "ctx", (1, 1))
    token_rows = seq_rows.reshape(seq_rows.shape[0] * seq_rows.shape[1], seq_rows.shape[2])
    shard_width = head_weight.shape[1]
    whole_rows = lax.all_gather(token_rows, VOCAB, axis=1, tiled=True)
    logits = jnp.dot(whole_rows, head_weight, preferred_element_type=jnp.float32)
    offset = lax.axis_index(CTX_VOCAB) * shard_width
    local_ids = ids_all.reshape(-1) - offset
    columns = jnp.arange(shard_width).astype(jnp.int32)
    onehot = (columns[None, :] == local_ids[:, None]).astype(jnp.float32)
    picked_part = jnp.sum(onehot * logits, axis=1)
    peak_part = jnp.max(logits, axis=1)
    row_peak = by_axis(peak_part, CTX_VOCAB)
    exp_sums = jnp.sum(jnp.exp(logits - row_peak[:, None]), axis=1)
    sum_total, picked = (by_axis_2(exp_sums, CTX_VOCAB), by_axis_2(picked_part, CTX_VOCAB))
    log_norm = row_peak + jnp.log(sum_total)
    mask_flat = mask_all.reshape(-1).astype(jnp.float32)
    seq_count = ids_all.shape[0]
    policy = jnp.sum(((picked - log_norm) * mask_flat).reshape(seq_count, ids_all.shape[1]), axis=1)
    log_ratio = policy - frozen_logprob
    pair_count = pair_order.shape[0] // 2
    chosen = pair_order[:pair_count]
    rejected = pair_order[pair_count:]
    margins = strength * (log_ratio[chosen] - log_ratio[rejected])
    pair_loss = jnp.mean(jax.nn.softplus(-margins))
    weight = -loss_scale * strength * jax.nn.sigmoid(-margins) / pair_count
    seq_coef = jnp.zeros((seq_count,), jnp.float32).at[chosen].set(weight).at[rejected].set(-weight)
    token_coef = (seq_coef[:, None] * mask_all.astype(jnp.float32)).reshape(-1)
    probabilities = jnp.exp(logits - log_norm[:, None])
    grad_logits = (token_coef[:, None] * (onehot - probabilities)).astype(jnp.bfloat16)
    spread_logits = (V / 64.0 * token_coef[:, None] * probabilities).astype(jnp.bfloat16)
    both_logits = jnp.concatenate([grad_logits, spread_logits], axis=1)
    both_grads = contract_rows(whole_rows, both_logits)
    head_grad = both_grads[:, :shard_width].astype(jnp.bfloat16)
    spread_grad = both_grads[:, shard_width:].astype(jnp.bfloat16)
    return (pair_loss, margins, head_grad, spread_grad)


def solution(mesh):
    split = Mesh(
        mesh.devices.reshape(mesh.shape["ctx"], 4, 4, 2), ("ctx", "vocab_0", "vocab_1", "vocab_2")
    )
    placed = (P(None, "ctx", VOCAB), P(None, CTX_VOCAB), P(None, "ctx"), P(None, "ctx"), P(), P())
    return jax.shard_map(
        shards,
        mesh=split,
        in_specs=placed,
        out_specs=(P(), P(), P(None, CTX_VOCAB), P(None, CTX_VOCAB)),
        check_vma=False,
    )
```

profile of v0, /device:TPU:1, one launch (start us, length us, event | category | flops | bytes accessed | tf_op | source)
XLA Modules:
  0.0 282.0 jit_solution(17380326910799111413)
XLA Ops:
  7.2 0.0 all-gather.4.cloned.1.call-start
  7.2 26.5 %all_gather.14 = bf16[16,128,128]{2,1,0:T(8,128)(2,1)} all-gather(bf16[16,16,128]{2,1,0:T(8,128)(2,1)} %param.6), channel_id=1, replica_groups=mesh['ctx'=8,'vocab_0'=4,'vocab_1'=4,'vocab_2'=2] {'ctx'}, dimensions={1}, use_global_device_ids=true | all-gather | bytes 589824 | tf_op jit(solution)/shard_map/all_gather | solution.py:49
  33.7 0.0 all-gather.4.cloned.1.call-update
  33.7 0.8 reshape.60
  34.5 0.8 reshape.61
  35.3 16.1 %all-gather.1 = s32[8,1,512]{2,1,0:T(1,128)S(1)} all-gather(s32[1,1,512]{2,1,0:T(1,128)S(1)} %bitcast.21), channel_id=2, replica_groups=mesh['ctx'=8,'vocab_0'=4,'vocab_1'=4,'vocab_2'=2] {'ctx'}, dimensions={0}, use_global_device_ids=true | all-gather | bytes 18432 | tf_op jit(solution)/shard_map/all_gather | solution.py:22
  51.4 0.1 sub.49
  51.5 0.1 sub.51
  51.6 0.1 convert_element_type.33
  51.7 0.1 convert_element_type.35
  51.8 0.8 compare_select_fusion.1
  52.6 71.6 %all-gather.4.cloned.1.call-done = bf16[2048,4096]{1,0:T(8,128)(2,1)} async-done(((bf16[2048,128]{1,0:T(8,128)(2,1)}), bf16[2048,4096]{1,0:T(8,128)(2,1)}) %all-gather.4.cloned.1.call-update) | async-done | bytes 16777232 | tf_op jit(solution)/shard_map/all_gather | solution.py:53
  124.2 14.8 %fusion.9 = (f32[2048]{0:T(1024)S(1)}, f32[2048,501]{0,1:T(8,128)}) fusion(bf16[2048,4096]{1,0:T(8,128)(2,1)} %all-gather.4.cloned.1.call-done, bf16[4096,501]{0,1:T(8,128)(2,1)} %param.7), kind=kOutput, calls=%fused_computation.35 | convolution fusion | flops 8406409216 | bytes 24993792 | tf_op jit(solution)/shard_map/dot_general | solution.py:54
  139.0 0.0 copy-start.1
  139.0 14.1 %pmax.28 = f32[2048]{0:T(1024)S(1)} all-reduce(f32[2048]{0:T(1024)S(1)} %get-tuple-element.29), channel_id=1, replica_groups=mesh['ctx'=8,'vocab_0'=4,'vocab_1'=4,'vocab_2'=2] {'ctx'}, use_global_device_ids=true, to_apply=%region_6.0 | all-reduce | flops 2048 | bytes 16384 | tf_op jit(solution)/shard_map/pmax | solution.py:32
  153.1 8.2 %pmax.29 = f32[2048]{0:T(1024)S(1)} all-reduce(f32[2048]{0:T(1024)S(1)} %pmax.28), channel_id=1, replica_groups=mesh['ctx'=8,'vocab_0'=4,'vocab_1'=4,'vocab_2'=2] {'vocab_0'}, use_global_device_ids=true, to_apply=%region_7.0 | all-reduce | flops 2048 | bytes 16384 | tf_op jit(solution)/shard_map/pmax | solution.py:32
  161.3 7.4 %pmax.30 = f32[2048]{0:T(1024)S(1)} all-reduce(f32[2048]{0:T(1024)S(1)} %pmax.29), channel_id=1, replica_groups=mesh['ctx'=8,'vocab_0'=4,'vocab_1'=4,'vocab_2'=2] {'vocab_1'}, use_global_device_ids=true, to_apply=%region_8.0 | all-reduce | flops 2048 | bytes 16384 | tf_op jit(solution)/shard_map/pmax | solution.py:32
  168.7 10.1 %pmax.31 = f32[2048]{0:T(1024)S(1)} all-reduce(f32[2048]{0:T(1024)S(1)} %pmax.30), channel_id=1, replica_groups=mesh['ctx'=8,'vocab_0'=4,'vocab_1'=4,'vocab_2'=2] {'vocab_2'}, use_global_device_ids=true, to_apply=%region_9.0 | all-reduce | flops 2048 | bytes 16384 | tf_op jit(solution)/shard_map/pmax | solution.py:32
  178.8 3.3 %exponential_reduce_fusion = (f32[2048]{0:T(1024)S(1)}, f32[2048]{0:T(1024)S(1)}) fusion(f32[2048,501]{0,1:T(8,128)} %get-tuple-element.30, f32[2048]{0:T(1024)S(1)} %pmax.31, s32[2048]{0:T(1024)S(1)} %sub.51), kind=kLoop, calls=%fused_computation.11 | loop fusion | flops 5126144 | bytes 4136960 | tf_op jit(solution)/shard_map/reduce_sum | solution.py:62
  182.1 20.5 %all-reduce = (f32[2048]{0:T(1024)S(1)}, f32[2048]{0:T(1024)S(1)}) all-reduce(f32[2048]{0:T(1024)S(1)} %get-tuple-element.5, f32[2048]{0:T(1024)S(1)} %get-tuple-element.4), channel_id=1, replica_groups=mesh['ctx'=8,'vocab_0'=4,'vocab_1'=4,'vocab_2'=2] {'ctx'}, use_global_device_ids=true, to_apply=%region_1.0 | all-reduce | flops 4096 | bytes 32768 | tf_op jit(solution)/shard_map/psum | solution.py:38
  202.6 10.8 %all-reduce.2 = (f32[2048]{0:T(1024)S(1)}, f32[2048]{0:T(1024)S(1)}) all-reduce(f32[2048]{0:T(1024)S(1)} %get-tuple-element.6, f32[2048]{0:T(1024)S(1)} %get-tuple-element.7), channel_id=1, replica_groups=mesh['ctx'=8,'vocab_0'=4,'vocab_1'=4,'vocab_2'=2] {'vocab_0'}, use_global_device_ids=true, to_apply=%region_2.0 | all-reduce | flops 4096 | bytes 32768 | tf_op jit(solution)/shard_map/psum | solution.py:38
  213.4 10.9 %all-reduce.1 = (f32[2048]{0:T(1024)S(1)}, f32[2048]{0:T(1024)S(1)}) all-reduce(f32[2048]{0:T(1024)S(1)} %get-tuple-element.10, f32[2048]{0:T(1024)S(1)} %get-tuple-element.11), channel_id=1, replica_groups=mesh['ctx'=8,'vocab_0'=4,'vocab_1'=4,'vocab_2'=2] {'vocab_1'}, use_global_device_ids=true, to_apply=%region_3.0 | all-reduce | flops 4096 | bytes 32768 | tf_op jit(solution)/shard_map/psum | solution.py:38
  224.3 17.9 %all-reduce.3 = (f32[2048]{0:T(1024)S(1)}, f32[2048]{0:T(1024)S(1)}) all-reduce(f32[2048]{0:T(1024)S(1)} %get-tuple-element.8, f32[2048]{0:T(1024)S(1)} %get-tuple-element.9), channel_id=1, replica_groups=mesh['ctx'=8,'vocab_0'=4,'vocab_1'=4,'vocab_2'=2] {'vocab_2'}, use_global_device_ids=true, to_apply=%region_4.0 | all-reduce | flops 4096 | bytes 32768 | tf_op jit(solution)/shard_map/psum | solution.py:38
  242.2 0.1 bitcast_reduce_fusion
  242.3 0.0 copy-done.1
  242.3 0.6 gather_fusion.1
  243.0 0.6 gather_fusion
  243.6 0.0 copy-start
  243.7 0.6 scatter_custom_fusion
  244.3 0.8 scatter_fusion
  245.1 0.1 broadcast_multiply_fusion
  245.1 3.5 %multiply_convert_fusion.1 = (bf16[2048,501]{0,1:T(8,128)(2,1)S(1)}, bf16[2048,501]{0,1:T(8,128)(2,1)S(1)}) fusion(f32[2048,501]{0,1:T(8,128)} %get-tuple-element.30, f32[2048]{0:T(1024)S(1)} %get-tuple-element.20, f32[2048]{0:T(1024)S(1)} %get-tuple-element.15, s32[2048]{0:T(1024)S(1)} %sub.51, f32[2048]{0:T(1024)S(1)} %get-tuple-element.14), kind=kLoop, calls=%fused_computation.9 | loop fusion | flops 8208384 | bytes 8241152 | tf_op jit(solution)/shard_map/convert_element_type | solution.py:78
  248.7 20.1 %convert_bitcast_fusion = bf16[4096,1002]{0,1:T(8,128)(2,1)S(1)} fusion(bf16[2048,4096]{1,0:T(8,128)(2,1)} %all-gather.4.cloned.1.call-done, bf16[2048,501]{0,1:T(8,128)(2,1)S(1)} %get-tuple-element.24, bf16[2048,501]{0,1:T(8,128)(2,1)S(1)} %get-tuple-element.23), kind=kOutput, calls=%fused_computation.4 | convolution fusion | flops 16823083008 | bytes 29089792 | tf_op jit(solution)/shard_map/dot_general | solution.py:43
  268.7 4.0 %fusion.8 = (bf16[4096,501]{0,1:T(8,128)(2,1)}, bf16[4096,501]{0,1:T(8,128)(2,1)}) fusion(bf16[4096,1002]{0,1:T(8,128)(2,1)S(1)} %convert_bitcast_fusion), kind=kLoop, calls=%fused_computation.34 | loop fusion | bytes 16416768 | tf_op jit(solution)/shard_map/slice | solution.py:83
  272.7 0.0 copy-done
  272.7 0.6 fusion.3
  (8 shorter events, 0.1 us)
Async XLA Ops:
  7.2 117.1 %all-gather.4.cloned.1.call-start = ((), (), s32[]{:S(2)}) async-start(), calls=%async_computation | async-start | bytes 17301504 | tf_op jit(solution)/shard_map/all_gather | solution.py:53
  139.0 103.3 %copy-start.1 = (f32[16]{0:T(128)S(1)}, f32[16]{0:T(128)}, u32[]{:S(2)}) copy-start(f32[16]{0:T(128)} %param.11) | copy-start | bytes 196
  243.6 29.1 %copy-start = (f32[8]{0:T(128)}, f32[8]{0:T(128)S(1)}, u32[]{:S(2)}) copy-start(f32[8]{0:T(128)S(1)} %get-tuple-element.18) | copy-start | bytes 100
Sparse Core Ops, SparseCore 0:
  33.8 90.3 all-gather.3
where the time goes:
time: 282 us
  blocking collectives  142 us (50%)
  waiting for transfers between devices  71.7 us (25%)
  matrix products  34.9 us (12%)
  between operations  15.9 us (6%)
  local copies, waits for them, and re-layouts  8.61 us (3%)
  other arithmetic  8.44 us (3%)
    all_gather x1, waiting for transfers between devices, shards(): whole_rows = lax.all_gather(token_rows, VOCAB, axis=1, tiled=True)  71.6 us
    psum x4, blocking collectives, by_axis_2(): shard = lax.psum(shard, axis)  60.1 us
    pmax x4, blocking collectives, by_axis(): shard = lax.pmax(shard, axis)  39.7 us
    all_gather x1, blocking collectives, shards(): seq_rows = lax.all_gather(hidden, 'ctx', axis=1, tiled=True)  26.5 us
    dot_general x1, matrix products, contract_rows(): lax.dot_general(block_rows, both_logits, (((0,), (0,)), ((), ())), prefer...  20.1 us
    all_gather x1, blocking collectives, gather_packed(): lines, at, finished = (lax.all_gather(flat, axis), 0, [])  16.1 us
    dot_general x1, matrix products, shards(): jnp.dot(whole_rows, head_weight, preferred_element_type=jnp.float32)  14.8 us
  transfers between devices with their start and end apart: 1, of which 1 were waited for; matrix products, arithmetic and copies ran while one was open for 1% of the time, Pallas kernels for 0%

commit v1 on v0

--- a/solution.py
+++ b/solution.py
@@ -9,6 +9,19 @@
 CTX_VOCAB = ("ctx", "vocab_0", "vocab_1", "vocab_2")
 strength = 0.1
 loss_scale = 256.0
+
+
+def ring_gather(x, axis, dim):
+    ways = lax.axis_size(axis)
+    up = [(d, (d + 1) % ways) for d in range(ways)]
+    down = [(d, (d - 1) % ways) for d in range(ways)]
+    earlier, later = ([x], [x])
+    for _ in range(ways // 2):
+        earlier.append(lax.ppermute(earlier[-1], axis, up))
+    for _ in range((ways - 1) // 2):
+        later.append(lax.ppermute(later[-1], axis, down))
+    line = jnp.concatenate([*earlier[::-1], *later[1:]], axis=dim)
+    return jnp.roll(line, (lax.axis_index(axis) - ways // 2) * x.shape[dim], axis=dim)
 
 
 def laid_out(pieces, dim):
@@ -46,7 +59,7 @@
 
 
 def shards(hidden, head_weight, token_ids, response_mask, pair_order, frozen_logprob):
-    seq_rows = lax.all_gather(hidden, "ctx", axis=1, tiled=True)
+    seq_rows = ring_gather(hidden, "ctx", 1)
     ids_all, mask_all = gather_packed((token_ids, response_mask), "ctx", (1, 1))
     token_rows = seq_rows.reshape(seq_rows.shape[0] * seq_rows.shape[1], seq_rows.shape[2])
     shard_width = head_weight.shape[1]

time: 282 us -> 280 us (level)
  blocking collectives: 142 us -> 117 us
  starting transfers between devices: 0.04 us -> 11 us
  waiting for transfers between devices: 71.7 us -> 81.6 us
    all_gather x1 -> x0, blocking collectives: 26.5 us -> none  [shards(): seq_rows = lax.all_gather(hidden, 'ctx', axis=1, tiled=True)]
    ppermute x0 -> x7, starting transfers between devices: none -> 11 us  [the longest x3 8.44 us: ring_gather(): later.append(lax.ppermute(later[-1], axis, down))]
    ppermute x0 -> x7, waiting for transfers between devices: none -> 10.3 us  [the longest x4 10.3 us: ring_gather(): earlier.append(lax.ppermute(earlier[-1], axis, up))]
  transfers between devices with their start and end apart: 1 -> 8, of which waited for: 1 -> 5; matrix products, arithmetic and copies ran while one was open for 1% -> 1% of each run, Pallas kernels for 0% -> 0%
where the time goes in v1:
time: 280 us; the launch traced here: 279 us
  blocking collectives  117 us (42%)
  waiting for transfers between devices  81.6 us (29%)
  matrix products  34.8 us (12%)
  between operations  16 us (6%)
  local copies, waits for them, and re-layouts  11.3 us (4%)
  starting transfers between devices  11 us (4%)
  other arithmetic  7.72 us (3%)
    all_gather x1, waiting for transfers between devices, shards(): whole_rows = lax.all_gather(token_rows, VOCAB, axis=1, tiled=True)  71.2 us
    psum x4, blocking collectives, by_axis_2(): shard = lax.psum(shard, axis)  60.1 us
    pmax x4, blocking collectives, by_axis(): shard = lax.pmax(shard, axis)  39.8 us
    dot_general x1, matrix products, contract_rows(): lax.dot_general(block_rows, both_logits, (((0,), (0,)), ((), ())), prefer...  20 us
    all_gather x1, blocking collectives, gather_packed(): lines, at, finished = (lax.all_gather(flat, axis), 0, [])  16.9 us
    dot_general x1, matrix products, shards(): jnp.dot(whole_rows, head_weight, preferred_element_type=jnp.float32)  14.8 us
    ppermute x4, waiting for transfers between devices, ring_gather(): earlier.append(lax.ppermute(earlier[-1], axis, up))  10.3 us
    ppermute x3, starting transfers between devices, ring_gather(): later.append(lax.ppermute(later[-1], axis, down))  8.44 us
  transfers between devices with their start and end apart: 8, of which 5 were waited for; matrix products, arithmetic and copies ran while one was open for 1% of the time, Pallas kernels for 0%

profile of v1, /device:TPU:1, one launch (start us, length us, event | category | flops | bytes accessed | tf_op | source)
XLA Modules:
  0.0 279.2 jit_solution(6724973408437147798)
XLA Ops:
  7.2 0.0 copy-start
  7.2 0.0 all-gather.4.cloned.1.call-start
  7.2 2.5 collective-permute-start
  9.8 5.8 %collective-permute-done = bf16[16,16,128]{2,1,0:T(8,128)(2,1)S(1)} collective-permute-done((bf16[16,16,128]{2,1,0:T(8,128)(2,1)}, bf16[16,16,128]{2,1,0:T(8,128)(2,1)S(1)}, u32[]{:S(2)}, u32[]{:S(2)}) %collective-permute-start) | collective-permute-done | bytes 65568 | tf_op jit(solution)/shard_map/ppermute | solution.py:20
  15.6 0.0 collective-permute-start.1
  15.6 2.7 collective-permute-start.4
  18.2 1.6 collective-permute-done.1
  19.9 0.0 collective-permute-start.2
  19.9 0.0 collective-permute-done.4
  19.9 2.9 %collective-permute-start.5 = (bf16[16,16,128]{2,1,0:T(8,128)(2,1)S(1)}, bf16[16,16,128]{2,1,0:T(8,128)(2,1)S(1)}, u32[]{:S(2)}, u32[]{:S(2)}) collective-permute-start(bf16[16,16,128]{2,1,0:T(8,128)(2,1)S(1)} %collective-permute-done.4), channel_id=1, source_target_pairs={{0,224},{32,0},{64,32},{96,64},{128,96},{160,128},{192,160},{224,1... | collective-permute-start | bytes 196616 | tf_op jit(solution)/shard_map/ppermute | solution.py:22
  22.8 1.4 collective-permute-done.2
  24.2 0.0 collective-permute-start.3
  24.2 0.0 collective-permute-done.5
  24.2 2.9 %collective-permute-start.6 = (bf16[16,16,128]{2,1,0:T(8,128)(2,1)S(1)}, bf16[16,16,128]{2,1,0:T(8,128)(2,1)S(1)}, u32[]{:S(2)}, u32[]{:S(2)}) collective-permute-start(bf16[16,16,128]{2,1,0:T(8,128)(2,1)S(1)} %collective-permute-done.5), channel_id=1, source_target_pairs={{0,224},{32,0},{64,32},{96,64},{128,96},{160,128},{192,160},{224,1... | collective-permute-start | bytes 196616 | tf_op jit(solution)/shard_map/ppermute | solution.py:22
  27.1 1.4 collective-permute-done.3
  28.6 0.9 constant_dynamic-update-slice_fusion.11
  29.5 0.0 collective-permute-done.6
  29.6 0.9 constant_dynamic-update-slice_fusion.3
  30.5 0.8 constant_dynamic-slice_fusion
  31.4 0.0 all-gather.4.cloned.1.call-update
  31.4 0.8 reshape.60
  32.2 0.8 reshape.61
  33.0 16.9 %all-gather.1 = s32[8,1,512]{2,1,0:T(1,128)S(1)} all-gather(s32[1,1,512]{2,1,0:T(1,128)S(1)} %bitcast.19), channel_id=2, replica_groups=mesh['ctx'=8,'vocab_0'=4,'vocab_1'=4,'vocab_2'=2] {'ctx'}, dimensions={0}, use_global_device_ids=true | all-gather | bytes 18432 | tf_op jit(solution)/shard_map/all_gather | solution.py:35
  49.8 0.1 sub.56
  50.0 0.1 sub.58
  50.0 0.1 convert_element_type.33
  50.2 0.1 convert_element_type.35
  50.2 0.0 copy-done
  50.3 0.1 compare_select_fusion.1
  50.3 71.2 %all-gather.4.cloned.1.call-done = bf16[2048,4096]{1,0:T(8,128)(2,1)} async-done(((bf16[2048,128]{1,0:T(8,128)(2,1)}), bf16[2048,4096]{1,0:T(8,128)(2,1)}) %all-gather.4.cloned.1.call-update) | async-done | bytes 16777232 | tf_op jit(solution)/shard_map/all_gather | solution.py:66
  121.5 14.8 %fusion.9 = (f32[2048]{0:T(1024)S(1)}, f32[2048,501]{0,1:T(8,128)}) fusion(bf16[2048,4096]{1,0:T(8,128)(2,1)} %all-gather.4.cloned.1.call-done, bf16[4096,501]{0,1:T(8,128)(2,1)} %param.7), kind=kOutput, calls=%fused_computation.52 | convolution fusion | flops 8406409216 | bytes 24993792 | tf_op jit(solution)/shard_map/dot_general | solution.py:67
  136.3 0.0 copy-start.2
  136.3 14.1 %pmax.28 = f32[2048]{0:T(1024)S(1)} all-reduce(f32[2048]{0:T(1024)S(1)} %get-tuple-element.29), channel_id=1, replica_groups=mesh['ctx'=8,'vocab_0'=4,'vocab_1'=4,'vocab_2'=2] {'ctx'}, use_global_device_ids=true, to_apply=%region_6.7 | all-reduce | flops 2048 | bytes 16384 | tf_op jit(solution)/shard_map/pmax | solution.py:45
  150.4 8.2 %pmax.29 = f32[2048]{0:T(1024)S(1)} all-reduce(f32[2048]{0:T(1024)S(1)} %pmax.28), channel_id=1, replica_groups=mesh['ctx'=8,'vocab_0'=4,'vocab_1'=4,'vocab_2'=2] {'vocab_0'}, use_global_device_ids=true, to_apply=%region_7.8 | all-reduce | flops 2048 | bytes 16384 | tf_op jit(solution)/shard_map/pmax | solution.py:45
  158.6 7.4 %pmax.30 = f32[2048]{0:T(1024)S(1)} all-reduce(f32[2048]{0:T(1024)S(1)} %pmax.29), channel_id=1, replica_groups=mesh['ctx'=8,'vocab_0'=4,'vocab_1'=4,'vocab_2'=2] {'vocab_1'}, use_global_device_ids=true, to_apply=%region_8.9 | all-reduce | flops 2048 | bytes 16384 | tf_op jit(solution)/shard_map/pmax | solution.py:45
  166.0 10.1 %pmax.31 = f32[2048]{0:T(1024)S(1)} all-reduce(f32[2048]{0:T(1024)S(1)} %pmax.30), channel_id=1, replica_groups=mesh['ctx'=8,'vocab_0'=4,'vocab_1'=4,'vocab_2'=2] {'vocab_2'}, use_global_device_ids=true, to_apply=%region_9.10 | all-reduce | flops 2048 | bytes 16384 | tf_op jit(solution)/shard_map/pmax | solution.py:45
  176.1 3.3 %exponential_reduce_fusion = (f32[2048]{0:T(1024)S(1)}, f32[2048]{0:T(1024)S(1)}) fusion(f32[2048,501]{0,1:T(8,128)} %get-tuple-element.30, f32[2048]{0:T(1024)S(1)} %pmax.31, s32[2048]{0:T(1024)S(1)} %sub.58), kind=kLoop, calls=%fused_computation.11 | loop fusion | flops 5126144 | bytes 4136960 | tf_op jit(solution)/shard_map/reduce_sum | solution.py:75
  179.4 20.5 %all-reduce = (f32[2048]{0:T(1024)S(1)}, f32[2048]{0:T(1024)S(1)}) all-reduce(f32[2048]{0:T(1024)S(1)} %get-tuple-element.5, f32[2048]{0:T(1024)S(1)} %get-tuple-element.4), channel_id=1, replica_groups=mesh['ctx'=8,'vocab_0'=4,'vocab_1'=4,'vocab_2'=2] {'ctx'}, use_global_device_ids=true, to_apply=%region_1.2 | all-reduce | flops 4096 | bytes 32768 | tf_op jit(solution)/shard_map/psum | solution.py:51
  199.9 10.8 %all-reduce.2 = (f32[2048]{0:T(1024)S(1)}, f32[2048]{0:T(1024)S(1)}) all-reduce(f32[2048]{0:T(1024)S(1)} %get-tuple-element.6, f32[2048]{0:T(1024)S(1)} %get-tuple-element.7), channel_id=1, replica_groups=mesh['ctx'=8,'vocab_0'=4,'vocab_1'=4,'vocab_2'=2] {'vocab_0'}, use_global_device_ids=true, to_apply=%region_2.3 | all-reduce | flops 4096 | bytes 32768 | tf_op jit(solution)/shard_map/psum | solution.py:51
  210.7 10.9 %all-reduce.1 = (f32[2048]{0:T(1024)S(1)}, f32[2048]{0:T(1024)S(1)}) all-reduce(f32[2048]{0:T(1024)S(1)} %get-tuple-element.10, f32[2048]{0:T(1024)S(1)} %get-tuple-element.11), channel_id=1, replica_groups=mesh['ctx'=8,'vocab_0'=4,'vocab_1'=4,'vocab_2'=2] {'vocab_1'}, use_global_device_ids=true, to_apply=%region_3.4 | all-reduce | flops 4096 | bytes 32768 | tf_op jit(solution)/shard_map/psum | solution.py:51
  221.6 17.9 %all-reduce.3 = (f32[2048]{0:T(1024)S(1)}, f32[2048]{0:T(1024)S(1)}) all-reduce(f32[2048]{0:T(1024)S(1)} %get-tuple-element.8, f32[2048]{0:T(1024)S(1)} %get-tuple-element.9), channel_id=1, replica_groups=mesh['ctx'=8,'vocab_0'=4,'vocab_1'=4,'vocab_2'=2] {'vocab_2'}, use_global_device_ids=true, to_apply=%region_4.5 | all-reduce | flops 4096 | bytes 32768 | tf_op jit(solution)/shard_map/psum | solution.py:51
  239.5 0.1 bitcast_reduce_fusion
  239.6 0.0 copy-done.2
  239.6 0.6 gather_fusion.1
  240.3 0.6 gather_fusion
  240.9 0.0 copy-start.1
  241.0 0.6 scatter_custom_fusion
  241.6 0.6 scatter_fusion
  242.2 0.1 broadcast_multiply_fusion
  242.2 3.5 %multiply_convert_fusion.1 = (bf16[2048,501]{0,1:T(8,128)(2,1)S(1)}, bf16[2048,501]{0,1:T(8,128)(2,1)S(1)}) fusion(f32[2048,501]{0,1:T(8,128)} %get-tuple-element.30, f32[2048]{0:T(1024)S(1)} %get-tuple-element.20, f32[2048]{0:T(1024)S(1)} %get-tuple-element.15, s32[2048]{0:T(1024)S(1)} %sub.58, f32[2048]{0:T(1024)S(1)} %get-tuple-element.14), kind=kLoop, calls=%fused_computation.9 | loop fusion | flops 8208384 | bytes 8241152 | tf_op jit(solution)/shard_map/convert_element_type | solution.py:91
  245.8 20.0 %convolution_convert_fusion = bf16[4096,1002]{0,1:T(8,128)(2,1)S(1)} fusion(bf16[2048,4096]{1,0:T(8,128)(2,1)} %all-gather.4.cloned.1.call-done, bf16[2048,501]{0,1:T(8,128)(2,1)S(1)} %get-tuple-element.24, bf16[2048,501]{0,1:T(8,128)(2,1)S(1)} %get-tuple-element.23), kind=kOutput, calls=%fused_computation.4 | convolution fusion | flops 16823083008 | bytes 29089792 | tf_op jit(solution)/shard_map/dot_general | solution.py:56
  265.8 4.1 %fusion.8 = (bf16[4096,501]{0,1:T(8,128)(2,1)}, bf16[4096,501]{0,1:T(8,128)(2,1)}) fusion(bf16[4096,1002]{0,1:T(8,128)(2,1)S(1)} %convolution_convert_fusion), kind=kLoop, calls=%fused_computation.51 | loop fusion | bytes 16416768 | tf_op jit(solution)/shard_map/slice | solution.py:96
  270.0 0.0 copy-done.1
  270.0 0.6 fusion.3
  (22 shorter events, 0.3 us)
Async XLA Ops:
  7.2 43.1 %copy-start = (s32[16]{0:T(128)S(1)}, s32[16]{0:T(128)}, u32[]{:S(2)}) copy-start(s32[16]{0:T(128)} %param.10) | copy-start | bytes 196
  7.2 114.4 %all-gather.4.cloned.1.call-start = ((), (), s32[]{:S(2)}) async-start(), calls=%async_computation | async-start | bytes 17301504 | tf_op jit(solution)/shard_map/all_gather | solution.py:66
  7.2 8.3 %collective-permute-start = (bf16[16,16,128]{2,1,0:T(8,128)(2,1)}, bf16[16,16,128]{2,1,0:T(8,128)(2,1)S(1)}, u32[]{:S(2)}, u32[]{:S(2)}) collective-permute-start(bf16[16,16,128]{2,1,0:T(8,128)(2,1)} %param.6), channel_id=1, source_target_pairs={{0,32},{32,64},{64,96},{96,128},{128,160},{160,192},{192,224},{224... | collective-permute-start | bytes 196616 | tf_op jit(solution)/shard_map/ppermute | solution.py:20
  15.6 4.3 %collective-permute-start.1 = (bf16[16,16,128]{2,1,0:T(8,128)(2,1)S(1)}, bf16[16,16,128]{2,1,0:T(8,128)(2,1)S(1)}, u32[]{:S(2)}, u32[]{:S(2)}) collective-permute-start(bf16[16,16,128]{2,1,0:T(8,128)(2,1)S(1)} %collective-permute-done), channel_id=1, source_target_pairs={{0,32},{32,64},{64,96},{96,128},{128,160},{160,192},{192,224},{224... | collective-permute-start | bytes 196616 | tf_op jit(solution)/shard_map/ppermute | solution.py:20
  15.6 4.3 %collective-permute-start.4 = (bf16[16,16,128]{2,1,0:T(8,128)(2,1)}, bf16[16,16,128]{2,1,0:T(8,128)(2,1)S(1)}, u32[]{:S(2)}, u32[]{:S(2)}) collective-permute-start(bf16[16,16,128]{2,1,0:T(8,128)(2,1)} %param.6), channel_id=1, source_target_pairs={{0,224},{32,0},{64,32},{96,64},{128,96},{160,128},{192,160},{224,1... | collective-permute-start | bytes 196616 | tf_op jit(solution)/shard_map/ppermute | solution.py:22
  19.9 4.3 %collective-permute-start.2 = (bf16[16,16,128]{2,1,0:T(8,128)(2,1)S(1)}, bf16[16,16,128]{2,1,0:T(8,128)(2,1)S(1)}, u32[]{:S(2)}, u32[]{:S(2)}) collective-permute-start(bf16[16,16,128]{2,1,0:T(8,128)(2,1)S(1)} %collective-permute-done.1), channel_id=1, source_target_pairs={{0,32},{32,64},{64,96},{96,128},{128,160},{160,192},{192,224},{224... | collective-permute-start | bytes 196616 | tf_op jit(solution)/shard_map/ppermute | solution.py:20
  19.9 4.3 %collective-permute-start.5 = (bf16[16,16,128]{2,1,0:T(8,128)(2,1)S(1)}, bf16[16,16,128]{2,1,0:T(8,128)(2,1)S(1)}, u32[]{:S(2)}, u32[]{:S(2)}) collective-permute-start(bf16[16,16,128]{2,1,0:T(8,128)(2,1)S(1)} %collective-permute-done.4), channel_id=1, source_target_pairs={{0,224},{32,0},{64,32},{96,64},{128,96},{160,128},{192,160},{224,1... | collective-permute-start | bytes 196616 | tf_op jit(solution)/shard_map/ppermute | solution.py:22
  24.2 4.3 %collective-permute-start.3 = (bf16[16,16,128]{2,1,0:T(8,128)(2,1)S(1)}, bf16[16,16,128]{2,1,0:T(8,128)(2,1)S(1)}, u32[]{:S(2)}, u32[]{:S(2)}) collective-permute-start(bf16[16,16,128]{2,1,0:T(8,128)(2,1)S(1)} %collective-permute-done.2), channel_id=1, source_target_pairs={{0,32},{32,64},{64,96},{96,128},{128,160},{160,192},{192,224},{224... | collective-permute-start | bytes 196616 | tf_op jit(solution)/shard_map/ppermute | solution.py:20
  24.2 5.3 %collective-permute-start.6 = (bf16[16,16,128]{2,1,0:T(8,128)(2,1)S(1)}, bf16[16,16,128]{2,1,0:T(8,128)(2,1)S(1)}, u32[]{:S(2)}, u32[]{:S(2)}) collective-permute-start(bf16[16,16,128]{2,1,0:T(8,128)(2,1)S(1)} %collective-permute-done.5), channel_id=1, source_target_pairs={{0,224},{32,0},{64,32},{96,64},{128,96},{160,128},{192,160},{224,1... | collective-permute-start | bytes 196616 | tf_op jit(solution)/shard_map/ppermute | solution.py:22
  136.3 103.3 %copy-start.2 = (f32[16]{0:T(128)S(1)}, f32[16]{0:T(128)}, u32[]{:S(2)}) copy-start(f32[16]{0:T(128)} %param.11) | copy-start | bytes 196
  240.9 29.0 %copy-start.1 = (f32[8]{0:T(128)}, f32[8]{0:T(128)S(1)}, u32[]{:S(2)}) copy-start(f32[8]{0:T(128)S(1)} %get-tuple-element.18) | copy-start | bytes 100
Sparse Core Ops, SparseCore 0:
  31.5 89.9 all-gather.3
